TPU v7x, 128 devices: a whole 4x4x4 slice. The times are simulated.
128 devices in a mesh: row: 8 (over y, core), col: 16 (over z, x).
Axes of the slice: x: 4, y: 4, z: 4, core: 2. Of those that a mesh axis runs over, the one named last changes fastest.
Arguments:
- images: bfloat16 [16384, 768], P(('row', 'col')), may hold values from -5 to 5
- texts: bfloat16 [16384, 768], P(('col', 'row')), may hold values from -5 to 5
- audio: bfloat16 [16384, 768], P(('col', 'row')), may hold values from -5 to 5
Outputs:
- grad_images: float32 [16384, 768], P(('row', 'col'))
- grad_texts: float32 [16384, 768], P(('col', 'row'))
- grad_audio: float32 [16384, 768], P(('col', 'row'))
All inputs are finite; a program needn't handle non-finite values.
Results may differ from a plain program's by a relative error of at most 0.013.
Values may be sent and summed in bfloat16 or wider, within the bound.
A program may use at most 128 MiB of HBM per device.

v0:
```python
import jax
import jax.numpy as jnp
from jax import lax
from jax.sharding import Mesh
from jax.sharding import PartitionSpec as P

ITERS = 3
COL = ("col_0", "col_1")
ROW_COL = ("row", "col_0", "col_1")
COL_ROW = ("col_0", "col_1", "row")
logit_softness = 0.07
target_softness = 0.05
epsilon = 1e-06


def in_one_piece(arrays, axis, dim, along):
    both = jnp.concatenate(arrays, axis=along)
    filled, at, outs = (lax.all_gather(both, axis, axis=dim, tiled=True), 0, [])
    for a in arrays:
        outs.append(lax.slice_in_dim(filled, at, at + a.shape[along], axis=along))
        at += a.shape[along]
    return tuple(outs)


def from_everyone(value, axis):
    size = lax.axis_size(axis)
    return lax.all_to_all(
        jnp.broadcast_to(value[None], (size, *value.shape)), axis, 0, 0, tiled=True
    )


def taken_together(value, axis):
    everything = from_everyone(value, axis)
    return jnp.sum(everything, axis=0)


def in_one(arrays, axis):
    ends = [0]
    for a in arrays:
        ends.append(ends[-1] + a.size)
    subtotal = taken_together(jnp.concatenate([a.ravel() for a in arrays]), axis)
    return tuple((subtotal[b:e].reshape(a.shape) for a, b, e in zip(arrays, ends, ends[1:])))


def summed_rows(terms, axes):
    subtotal = terms.astype(jnp.bfloat16)
    for axis in axes:
        subtotal = lax.psum_scatter(subtotal, axis, scatter_dimension=0, tiled=True)
    return subtotal.astype(jnp.float32)


def cut_along(value, dim, size):
    shape = value.shape
    blocks = value.reshape(*shape[:dim], size, shape[dim] // size, *shape[dim + 1 :])
    return jnp.moveaxis(blocks, dim, 0)


def summed_on_arrival(value, axis, dim):
    blocks = cut_along(value, dim, lax.axis_size(axis))
    arrived = lax.all_to_all(blocks, axis, split_axis=0, concat_axis=0, tiled=True)
    return arrived.astype(jnp.float32).sum(axis=0)


def normalize(raw):
    values = raw.astype(jnp.float32)
    inverse = lax.rsqrt(jnp.sum(values * values, axis=1, keepdims=True) + epsilon)
    return (values * inverse, inverse)


def backward(unit, inverse, incoming):
    return (incoming - unit * jnp.sum(unit * incoming, axis=1, keepdims=True)) * inverse


def shards(images, texts, audio):
    img_unit, img_inverse = normalize(images)
    txt_unit, txt_inverse = normalize(texts)
    aud_unit, aud_inverse = normalize(audio)
    img_rows = lax.all_gather(img_unit.astype(jnp.bfloat16), COL, axis=0, tiled=True)
    text_columns, audio_columns = in_one_piece(
        (txt_unit.astype(jnp.bfloat16), aud_unit.astype(jnp.bfloat16)), "row", 0, 1
    )
    paired_cols = jnp.concatenate([text_columns, audio_columns], axis=0)
    contract = (((1,), (1,)), ((), ()))
    cosine_matrix = lax.dot_general(
        img_rows, paired_cols, contract, preferred_element_type=jnp.float32
    )
    row_extent = img_rows.shape[0]
    column_width = text_columns.shape[0]
    loss_routine = jnp.exp(cosine_matrix / target_softness).reshape(row_extent, 2, column_width)
    softmax_exponent = jnp.exp(cosine_matrix / logit_softness).reshape(row_extent, 2, column_width)
    cols_scale = jnp.ones((2, column_width), jnp.float32)
    opening = 0
    row_sums, row_total = in_one(
        (jnp.sum(loss_routine * cols_scale[None], axis=2), jnp.sum(softmax_exponent, axis=2)), COL
    )
    rows_scale = 1.0 / row_sums
    col_sums, col_total = in_one(
        (jnp.sum(loss_routine * rows_scale[:, :, None], axis=0), jnp.sum(softmax_exponent, axis=0)),
        "row",
    )
    cols_scale = 1.0 / col_sums
    opening = 1
    for iteration in range(opening, ITERS):
        row_sums = taken_together(jnp.sum(loss_routine * cols_scale[None], axis=2), COL)
        rows_scale = 1.0 / row_sums
        col_sums = taken_together(jnp.sum(loss_routine * rows_scale[:, :, None], axis=0), "row")
        cols_scale = 1.0 / col_sums
    target = loss_routine * rows_scale[:, :, None] * cols_scale[None]
    row_mass = taken_together(jnp.sum(target, axis=2), COL)
    score_grad = (
        softmax_exponent / row_total[:, :, None] * row_mass[:, :, None]
        - target
        + softmax_exponent / col_total[None]
        - target
    )
    score_matrix = score_grad.astype(jnp.bfloat16).reshape(row_extent, 2 * column_width)
    owned = images.shape[0]
    image_gradient = summed_rows(
        jnp.dot(score_matrix, paired_cols, preferred_element_type=jnp.float32) / logit_softness, COL
    )
    text_part = lax.slice_in_dim(score_matrix, 0, owned * lax.axis_size("row"), axis=1)
    audio_part = lax.dynamic_slice_in_dim(
        score_matrix, column_width, owned * lax.axis_size("row"), 1
    )
    down = (((0,), (0,)), ((), ()))
    text_gradient_out = lax.dot_general(
        text_part, img_rows, down, preferred_element_type=jnp.float32
    )
    audio_gradient_out = lax.dot_general(
        audio_part, img_rows, down, preferred_element_type=jnp.float32
    )
    paired_grad = summed_on_arrival(
        (jnp.concatenate([text_gradient_out, audio_gradient_out], axis=1) / logit_softness).astype(
            jnp.bfloat16
        ),
        "row",
        0,
    )
    width = images.shape[1]
    grad_txt = backward(txt_unit, txt_inverse, paired_grad[:, :width])
    grad_aud = backward(aud_unit, aud_inverse, paired_grad[:, width:])
    return (backward(img_unit, img_inverse, image_gradient), grad_txt, grad_aud)


def solution(mesh):
    split = Mesh(mesh.devices.reshape(mesh.shape["row"], 4, 4), ("row", "col_0", "col_1"))
    placed = (P(ROW_COL, None), P(COL_ROW, None), P(COL_ROW, None))
    return jax.shard_map(
        shards,
        mesh=split,
        in_specs=placed,
        out_specs=(P(ROW_COL, None), P(COL_ROW, None), P(COL_ROW, None)),
        check_vma=False,
    )
```

profile of v0, /device:TPU:0, one launch (start us, length us, event | category | flops | bytes accessed | tf_op | source)
XLA Modules:
  0.0 329.2 jit_solution(17503242842045232137)
XLA Ops:
  7.2 0.0 all-gather.5.cloned.1.call-start
  7.2 1.0 fusion.30
  8.3 1.1 fusion.34
  9.3 1.2 fusion.20
  10.5 0.8 pad_maximum_fusion.3
  11.3 0.0 all-gather.3.cloned.1.call-start
  11.3 1.0 fusion.26
  12.4 1.7 fusion.25
  14.1 0.0 all-gather.3.cloned.1.call-update
  14.1 27.5 %all-gather.5.cloned.1.call-done = bf16[1024,1536]{1,0:T(8,128)(2,1)} async-done(((bf16[128,1536]{1,0:T(8,128)(2,1)}), bf16[1024,1536]{1,0:T(8,128)(2,1)}) %all-gather.5.cloned.1.call-update) | async-done | bytes 3145744 | tf_op jit(solution)/shard_map/all_gather | solution.py:18
  41.6 3.2 fusion.39
  44.9 47.4 %all-gather.3.cloned.1.call-done = bf16[2048,768]{1,0:T(8,128)(2,1)} async-done(((bf16[128,768]{1,0:T(8,128)(2,1)}), bf16[2048,768]{1,0:T(8,128)(2,1)}) %all-gather.3.cloned.1.call-update) | async-done | bytes 3145744 | tf_op jit(solution)/shard_map/all_gather | solution.py:78
  92.2 14.3 %bitcast_reduce_fusion.1 = (f32[2048,2]{0,1:T(2,128)S(1)}, f32[2048,2]{0,1:T(2,128)S(1)}, f32[2048,2048]{0,1:T(8,128)}) fusion(bf16[2048,768]{1,0:T(8,128)(2,1)} %all-gather.3.cloned.1.call-done, bf16[1024,768]{1,0:T(8,128)(2,1)} %get-tuple-element.10, bf16[1024,768]{1,0:T(8,128)(2,1)S(1)} %get-tuple-element.9), kind=kOutput, calls=%fused_computation.15 | convolution fusion | flops 6465511424 | bytes 23101440 | tf_op jit(solution)/shard_map/dot_general | solution.py:84
  106.5 0.4 copy.16
  106.9 0.5 reshape.133
  107.3 0.4 copy.17
  107.7 0.5 reshape.135
  108.2 0.4 broadcast_in_dim.18
  108.6 15.1 %all_to_all.42 = f32[16,1,8192]{2,1,0:T(1,128)S(1)} all-to-all(f32[16,1,8192]{2,1,0:T(1,128)S(1)} %broadcast_in_dim.18), channel_id=1, replica_groups=mesh['row'=8,'col_0'=4,'col_1'=4] {'col_0','col_1'}, dimensions={0} | all-to-all | bytes 1048576 | tf_op jit(solution)/shard_map/all_to_all | solution.py:27
  123.7 0.3 reduce_sum.212
  124.0 1.0 div.96
  125.0 0.3 copy.20
  125.4 8.5 %fusion.5 = (f32[2048]{0:T(1024)S(1)}, f32[2048]{0:T(1024)S(1)}) fusion(f32[2048,2]{0,1:T(2,128)S(1)} %copy.20, f32[2048,2048]{0,1:T(8,128)} %get-tuple-element.17), kind=kLoop, calls=%fused_computation.9 | loop fusion | flops 20967424 | bytes 16809984 | tf_op jit(solution)/shard_map/reduce_sum | solution.py:98
  133.9 0.1 broadcast_in_dim.19
  134.0 10.2 %all_to_all.43 = f32[8,1,4096]{2,1,0:T(1,128)S(1)} all-to-all(f32[8,1,4096]{2,1,0:T(1,128)S(1)} %broadcast_in_dim.19), channel_id=1, replica_groups=mesh['row'=8,'col_0'=4,'col_1'=4] {'row'}, dimensions={0} | all-to-all | bytes 262144 | tf_op jit(solution)/shard_map/all_to_all | solution.py:27
  144.2 0.1 reduce_sum.215
  144.3 7.4 %fusion.6 = f32[2048,2]{0,1:T(2,128)S(1)} fusion(f32[2,1024]{1,0:T(2,128)S(1)} %div.98, f32[2048,2048]{0,1:T(8,128)} %get-tuple-element.17), kind=kLoop, calls=%fused_computation.16 | loop fusion | flops 12578816 | bytes 16801792 | tf_op jit(solution)/shard_map/reduce_sum | solution.py:104
  151.7 0.1 broadcast_in_dim.20
  151.8 11.6 %all_to_all.44 = f32[16,2048,2]{1,2,0:T(2,128)S(1)} all-to-all(f32[16,2048,2]{1,2,0:T(2,128)S(1)} %broadcast_in_dim.20), channel_id=1, replica_groups=mesh['row'=8,'col_0'=4,'col_1'=4] {'col_0','col_1'}, dimensions={0} | all-to-all | bytes 524288 | tf_op jit(solution)/shard_map/all_to_all | solution.py:27
  163.4 0.1 reduce_sum.217
  163.5 8.6 %fusion.4 = f32[2048]{0:T(1024)S(1)} fusion(f32[2048,2]{0,1:T(2,128)S(1)} %broadcast_divide_fusion.1, f32[2048,2048]{0,1:T(8,128)} %get-tuple-element.17), kind=kLoop, calls=%fused_computation.7 | loop fusion | flops 12580864 | bytes 16801792 | tf_op jit(solution)/shard_map/reduce_sum | solution.py:106
  172.2 8.0 %all_to_all.45 = f32[8,2,1024]{2,1,0:T(2,128)S(1)} all-to-all(f32[8,2,1024]{2,1,0:T(2,128)S(1)} %broadcast_in_dim.22), channel_id=1, replica_groups=mesh['row'=8,'col_0'=4,'col_1'=4] {'row'}, dimensions={0} | all-to-all | bytes 131072 | tf_op jit(solution)/shard_map/all_to_all | solution.py:27
  180.2 7.4 %fusion.7 = f32[2048,2]{0,1:T(2,128)S(1)} fusion(f32[2,1024]{1,0:T(2,128)S(1)} %broadcast_divide_fusion.3, f32[2048,2048]{0,1:T(8,128)} %get-tuple-element.17), kind=kLoop, calls=%fused_computation.17 | loop fusion | flops 12578816 | bytes 16801792 | tf_op jit(solution)/shard_map/reduce_sum | solution.py:104
  187.6 0.1 broadcast_in_dim.23
  187.7 11.6 %all_to_all.46 = f32[16,2048,2]{1,2,0:T(2,128)S(1)} all-to-all(f32[16,2048,2]{1,2,0:T(2,128)S(1)} %broadcast_in_dim.23), channel_id=1, replica_groups=mesh['row'=8,'col_0'=4,'col_1'=4] {'col_0','col_1'}, dimensions={0} | all-to-all | bytes 524288 | tf_op jit(solution)/shard_map/all_to_all | solution.py:27
  199.3 0.1 reduce_sum.221
  199.4 8.6 %fusion.10 = f32[2048]{0:T(1024)S(1)} fusion(f32[2048,2]{0,1:T(2,128)S(1)} %broadcast_divide_fusion, f32[2048,2048]{0,1:T(8,128)} %get-tuple-element.17), kind=kLoop, calls=%fused_computation.22 | loop fusion | flops 12580864 | bytes 16801792 | tf_op jit(solution)/shard_map/reduce_sum | solution.py:106
  208.0 8.0 %all_to_all.47 = f32[8,2,1024]{2,1,0:T(2,128)S(1)} all-to-all(f32[8,2,1024]{2,1,0:T(2,128)S(1)} %broadcast_in_dim.25), channel_id=1, replica_groups=mesh['row'=8,'col_0'=4,'col_1'=4] {'row'}, dimensions={0} | all-to-all | bytes 131072 | tf_op jit(solution)/shard_map/all_to_all | solution.py:27
  216.0 7.6 %fusion.9 = f32[2048,2]{0,1:T(2,128)S(1)} fusion(f32[2,1024]{1,0:T(2,128)S(1)} %broadcast_divide_fusion.2, f32[2048,2]{0,1:T(2,128)S(1)} %broadcast_divide_fusion, f32[2048,2048]{0,1:T(8,128)} %get-tuple-element.17), kind=kLoop, calls=%fused_computation.19 | loop fusion | flops 16773120 | bytes 16818176 | tf_op jit(solution)/shard_map/reduce_sum | solution.py:109
  223.7 0.8 broadcast_in_dim.26
  224.5 3.5 %all-to-all-start.6 = ((f32[16,2048,2]{1,2,0:T(2,128)}), f32[16,2048,2]{1,2,0:T(2,128)S(1)}, u32[]{:S(2)}, u32[]{:S(2)}) async-start(f32[16,2048,2]{1,2,0:T(2,128)} %broadcast_in_dim.26), calls=%async_computation.6 | async-start | bytes 524288 | tf_op jit(solution)/shard_map/all_to_all | solution.py:27
  228.0 0.3 reduce-scatter.3.cloned.1.call-start
  228.3 1.0 slice.58
  229.3 0.3 copy.19
  229.6 7.2 %all-to-all-done.6 = f32[16,2048,2]{1,2,0:T(2,128)S(1)} async-done(((f32[16,2048,2]{1,2,0:T(2,128)}), f32[16,2048,2]{1,2,0:T(2,128)S(1)}, u32[]{:S(2)}, u32[]{:S(2)}) %all-to-all-start.6) | async-done | bytes 262176 | tf_op jit(solution)/shard_map/all_to_all | solution.py:27
  236.8 0.1 reduce_sum.225
  236.9 12.1 %fusion.3 = bf16[2048,2048]{0,1:T(8,128)(2,1)S(1)} fusion(f32[2048,2048]{0,1:T(8,128)} %get-tuple-element.17, f32[2048]{0:T(1024)S(1)} %get-tuple-element.16, f32[2048]{0:T(1024)S(1)} %bitcast.56, f32[2048,2]{0,1:T(2,128)S(1)} %reduce_sum.225, f32[2048,2]{0,1:T(2,128)S(1)} %broadcast_divide_fusion, f32[2048,2]{0,1:T(2,128)S(1)} %copy.19), kind=kLoop, calls=%fused_computation.4 | loop fusion | flops 46137344 | bytes 25231360 | tf_op jit(solution)/shard_map/convert_element_type | solution.py:116
  249.0 3.2 copy-done
  252.2 8.5 %multiply_convert_fusion = bf16[2048,768]{1,0:T(8,128)(2,1)} fusion(bf16[2048,2048]{0,1:T(8,128)(2,1)S(1)} %fusion.3, bf16[1024,768]{1,0:T(8,128)(2,1)S(1)} %copy-done.4, bf16[1024,768]{1,0:T(8,128)(2,1)S(1)} %get-tuple-element.9), kind=kOutput, calls=%fused_computation.27 | convolution fusion | flops 6451888128 | bytes 14680064 | tf_op jit(solution)/shard_map/dot_general | solution.py:119
  260.8 6.3 %fusion.13 = f32[1024,768]{1,0:T(8,128)S(1)} fusion(bf16[2048,768]{1,0:T(8,128)(2,1)} %all-gather.3.cloned.1.call-done, bf16[2048,2048]{0,1:T(8,128)(2,1)} %copy-done), kind=kOutput, calls=%fused_computation.28 | convolution fusion | flops 3221225472 | bytes 10485760 | tf_op jit(solution)/shard_map/dot_general | solution.py:129
  267.1 0.7 copy-done.5
  267.9 3.4 %fusion.15 = f32[1024,768]{1,0:T(8,128)S(1)} fusion(bf16[2048,768]{1,0:T(8,128)(2,1)S(1)} %copy-done.5, bf16[2048,2048]{0,1:T(8,128)(2,1)S(1)} %copy-done.1), kind=kOutput, calls=%fused_computation.30 | convolution fusion | flops 3221225472 | bytes 10485760 | tf_op jit(solution)/shard_map/dot_general | solution.py:126
  271.3 2.3 fusion.12
  273.6 3.6 %all-to-all-start.7 = ((bf16[8,128,1536]{2,1,0:T(8,128)(2,1)}), bf16[8,128,1536]{2,1,0:T(8,128)(2,1)S(1)}, u32[]{:S(2)}, u32[]{:S(2)}) async-start(bf16[8,128,1536]{2,1,0:T(8,128)(2,1)} %fusion.12), calls=%async_computation.9 | async-start | bytes 6291456 | tf_op jit(solution)/shard_map/all_to_all | solution.py:60
  277.3 0.0 reduce-scatter.5.cloned.1.call-start
  277.4 17.7 %reduce-scatter.3.cloned.1.call-done = bf16[512,768]{1,0:T(8,128)(2,1)} async-done(((bf16[2048,768]{1,0:T(8,128)(2,1)}), bf16[512,768]{1,0:T(8,128)(2,1)}) %reduce-scatter.3.cloned.1.call-update) | async-done | bytes 786448 | tf_op jit(solution)/shard_map/reduce_scatter | solution.py:48
  295.1 0.0 reduce-scatter.5.cloned.1.call-update
  295.1 20.6 %all-to-all-done.7 = bf16[8,128,1536]{2,1,0:T(8,128)(2,1)S(1)} async-done(((bf16[8,128,1536]{2,1,0:T(8,128)(2,1)}), bf16[8,128,1536]{2,1,0:T(8,128)(2,1)S(1)}, u32[]{:S(2)}, u32[]{:S(2)}) %all-to-all-start.7) | async-done | bytes 3145760 | tf_op jit(solution)/shard_map/all_to_all | solution.py:60
  315.6 0.4 convert_reduce_fusion
  316.1 0.3 fusion.31
  316.3 1.1 fusion.33
  317.4 2.0 reduce-scatter.5.cloned.1.call-done
  319.4 1.2 fusion.35
  320.6 2.0 fusion.36
  (32 shorter events, 0.3 us)
Async XLA Ops:
  7.2 34.5 %all-gather.5.cloned.1.call-start = ((), (), s32[]{:S(2)}) async-start(), calls=%async_computation.11 | async-start | bytes 3538944 | tf_op jit(solution)/shard_map/all_gather | solution.py:18
  11.3 80.9 %all-gather.3.cloned.1.call-start = ((), (), s32[]{:S(2)}) async-start(), calls=%async_computation.10 | async-start | bytes 3342336 | tf_op jit(solution)/shard_map/all_gather | solution.py:78
  224.5 12.4 %all-to-all-start.6 = ((f32[16,2048,2]{1,2,0:T(2,128)}), f32[16,2048,2]{1,2,0:T(2,128)S(1)}, u32[]{:S(2)}, u32[]{:S(2)}) async-start(f32[16,2048,2]{1,2,0:T(2,128)} %broadcast_in_dim.26), calls=%async_computation.6 | async-start | bytes 524288 | tf_op jit(solution)/shard_map/all_to_all | solution.py:27
  228.0 67.1 %reduce-scatter.3.cloned.1.call-start = ((), (), s32[]{:S(2)}) async-start(), calls=%async_computation.12 | async-start | bytes 3932160 | tf_op jit(solution)/shard_map/reduce_scatter | solution.py:48
  236.9 15.3 %copy-start.4 = (bf16[1024,768]{1,0:T(8,128)(2,1)S(1)}, bf16[1024,768]{1,0:T(8,128)(2,1)}, u32[]{:S(2)}) copy-start(bf16[1024,768]{1,0:T(8,128)(2,1)} %get-tuple-element.10) | copy-start | bytes 4718596
  249.0 3.2 copy-start
  260.8 6.3 %copy-start.1 = (bf16[2048,2048]{0,1:T(8,128)(2,1)S(1)}, bf16[2048,2048]{0,1:T(8,128)(2,1)}, u32[]{:S(2)}) copy-start(bf16[2048,2048]{0,1:T(8,128)(2,1)} %copy-done) | copy-start | bytes 25165828
  260.8 7.0 %copy-start.5 = (bf16[2048,768]{1,0:T(8,128)(2,1)S(1)}, bf16[2048,768]{1,0:T(8,128)(2,1)}, u32[]{:S(2)}) copy-start(bf16[2048,768]{1,0:T(8,128)(2,1)} %all-gather.3.cloned.1.call-done) | copy-start | bytes 9437188
  271.3 44.8 %copy-start.2 = (bf16[128,768]{1,0:T(8,128)(2,1)S(1)}, bf16[128,768]{1,0:T(8,128)(2,1)}, u32[]{:S(2)}) copy-start(bf16[128,768]{1,0:T(8,128)(2,1)} %param.5) | copy-start | bytes 589828
  271.3 44.8 %copy-start.3 = (bf16[128,768]{1,0:T(8,128)(2,1)S(1)}, bf16[128,768]{1,0:T(8,128)(2,1)}, u32[]{:S(2)}) copy-start(bf16[128,768]{1,0:T(8,128)(2,1)} %param.4) | copy-start | bytes 589828
  273.6 42.0 %all-to-all-start.7 = ((bf16[8,128,1536]{2,1,0:T(8,128)(2,1)}), bf16[8,128,1536]{2,1,0:T(8,128)(2,1)S(1)}, u32[]{:S(2)}, u32[]{:S(2)}) async-start(bf16[8,128,1536]{2,1,0:T(8,128)(2,1)} %fusion.12), calls=%async_computation.9 | async-start | bytes 6291456 | tf_op jit(solution)/shard_map/all_to_all | solution.py:60
  277.3 42.1 %reduce-scatter.5.cloned.1.call-start = ((), (), s32[]{:S(2)}) async-start(), calls=%async_computation.13 | async-start | bytes 983040 | tf_op jit(solution)/shard_map/reduce_scatter | solution.py:48
Sparse Core Ops, SparseCore 0:
  11.4 30.1 all-gather.4
  44.3 47.8 all-gather.2
  260.9 34.0 reduce-scatter.2
  297.3 22.0 reduce-scatter.4
where the time goes:
time: 330 us; the launch traced here: 329 us
  waiting for transfers between devices  122 us (37%)
  other arithmetic  75.1 us (23%)
  blocking collectives  64.5 us (20%)
  matrix products  32.5 us (10%)
  between operations  14.1 us (4%)
  local copies, waits for them, and re-layouts  13.1 us (4%)
  starting transfers between devices  7.57 us (2%)
    all_to_all x6, blocking collectives, from_everyone(): lax.all_to_all(jnp.broadcast_to(value[None], (size, *value.shape)), axis,...  64.5 us
    all_gather x1, waiting for transfers between devices, shards(): lax.all_gather(img_unit.astype(jnp.bfloat16), COL, axis=0, tiled=True)  47.4 us
    all_gather x1, waiting for transfers between devices, in_one_piece(): filled, at, outs = (lax.all_gather(both, axis, axis=dim, tiled=True), 0, [])  27.5 us
    reduce_sum x3, other arithmetic, shards(): jnp.sum(loss_routine * rows_scale[:, :, None], axis=0)  25.7 us
    all_to_all x1, waiting for transfers between devices, summed_on_arrival(): lax.all_to_all(blocks, axis, split_axis=0, concat_axis=0, tiled=True)  20.6 us
    reduce_scatter x2, waiting for transfers between devices, summed_rows(): subtotal = lax.psum_scatter(subtotal, axis, scatter_dimension=0, tiled=True)  19.7 us
    reduce_sum x2, other arithmetic, shards(): jnp.sum(loss_routine * cols_scale[None], axis=2)  14.7 us
    dot_general x1, matrix products, shards(): lax.dot_general(img_rows, paired_cols, contract, preferred_element_type=j...  14.3 us
  transfers between devices with their start and end apart: 6, of which 6 were waited for; matrix products, arithmetic and copies ran while one was open for 6% of the time, Pallas kernels for 0%

commit v1 on v0

--- a/solution.py
+++ b/solution.py
@@ -75,7 +75,10 @@
     img_unit, img_inverse = normalize(images)
     txt_unit, txt_inverse = normalize(texts)
     aud_unit, aud_inverse = normalize(audio)
-    img_rows = lax.all_gather(img_unit.astype(jnp.bfloat16), COL, axis=0, tiled=True)
+    img_rows = jnp.concatenate(
+        lax.all_to_all(jnp.stack([img_unit.astype(jnp.bfloat16)] * lax.axis_size(COL)), COL, 0, 0),
+        axis=0,
+    )
     text_columns, audio_columns = in_one_piece(
         (txt_unit.astype(jnp.bfloat16), aud_unit.astype(jnp.bfloat16)), "row", 0, 1
     )

time: 330 us -> 309 us (0.936)
  waiting for transfers between devices: 122 us -> 90.7 us
  starting transfers between devices: 7.57 us -> 15.5 us
  local copies, waits for them, and re-layouts: 13.1 us -> 19.3 us
    all_gather x1 -> x0, waiting for transfers between devices: 47.4 us -> none  [shards(): lax.all_gather(img_unit.astype(jnp.bfloat16), COL, axis=0, tiled=True)]
    all_to_all x0 -> x1, waiting for transfers between devices: none -> 25.6 us  [shards(): lax.all_to_all(jnp.stack([img_unit.astype(jnp.bfloat16)] * lax.axis_size(...]
    all_gather x1, waiting for transfers between devices: 27.5 us -> 18.2 us  [in_one_piece(): filled, at, outs = (lax.all_gather(both, axis, axis=dim, tiled=True), 0, [])]
    all_to_all x0 -> x1, starting transfers between devices: none -> 7.99 us  [shards(): lax.all_to_all(jnp.stack([img_unit.astype(jnp.bfloat16)] * lax.axis_size(...]
    slice x0 -> x1, local copies, waits for them, and re-layouts: none -> 4.4 us  [shards(): lax.slice_in_dim(score_matrix, 0, owned * lax.axis_size('row'), axis=1)]
  transfers between devices with their start and end apart: 6 -> 6, of which waited for: 6 -> 6; matrix products, arithmetic and copies ran while one was open for 6% -> 8% of each run, Pallas kernels for 0% -> 0%
where the time goes in v1:
time: 309 us; the launch traced here: 308 us
  waiting for transfers between devices  90.7 us (29%)
  other arithmetic  74.5 us (24%)
  blocking collectives  64.2 us (21%)
  matrix products  29.9 us (10%)
  local copies, waits for them, and re-layouts  19.3 us (6%)
  starting transfers between devices  15.5 us (5%)
  between operations  14.1 us (5%)
    all_to_all x6, blocking collectives, from_everyone(): lax.all_to_all(jnp.broadcast_to(value[None], (size, *value.shape)), axis,...  64.2 us
    reduce_sum x3, other arithmetic, shards(): jnp.sum(loss_routine * rows_scale[:, :, None], axis=0)  25.7 us
    all_to_all x1, waiting for transfers between devices, shards(): lax.all_to_all(jnp.stack([img_unit.astype(jnp.bfloat16)] * lax.axis_size(...  25.6 us
    all_to_all x1, waiting for transfers between devices, summed_on_arrival(): lax.all_to_all(blocks, axis, split_axis=0, concat_axis=0, tiled=True)  21.4 us
    all_gather x1, waiting for transfers between devices, in_one_piece(): filled, at, outs = (lax.all_gather(both, axis, axis=dim, tiled=True), 0, [])  18.2 us
    reduce_scatter x2, waiting for transfers between devices, summed_rows(): subtotal = lax.psum_scatter(subtotal, axis, scatter_dimension=0, tiled=True)  18.2 us
    reduce_sum x2, other arithmetic, shards(): jnp.sum(loss_routine * cols_scale[None], axis=2)  14.7 us
    dot_general x1, matrix products, shards(): lax.dot_general(img_rows, paired_cols, contract, preferred_element_type=j...  14.5 us
  transfers between devices with their start and end apart: 6, of which 6 were waited for; matrix products, arithmetic and copies ran while one was open for 8% of the time, Pallas kernels for 0%

profile of v1, /device:TPU:0, one launch (start us, length us, event | category | flops | bytes accessed | tf_op | source)
XLA Modules:
  0.0 308.2 jit_solution(10593426790250327959)
XLA Ops:
  7.2 0.0 all-gather.2.cloned.1.call-start
  7.2 1.0 fusion.26
  8.3 1.1 fusion.30
  9.3 1.2 fusion.16
  10.5 0.8 pad_maximum_fusion.3
  11.3 0.0 all-gather.2.cloned.1.call-update
  11.3 1.0 fusion.22
  12.3 1.0 fusion.21
  13.4 2.0 stack.2
  15.4 8.0 %all-to-all-start = ((bf16[16,128,768]{2,1,0:T(8,128)(2,1)}), bf16[16,128,768]{2,1,0:T(8,128)(2,1)S(1)}, u32[]{:S(2)}, u32[]{:S(2)}) async-start(bf16[16,128,768]{2,1,0:T(8,128)(2,1)} %stack.2), calls=%async_computation | async-start | bytes 6291456 | tf_op jit(solution)/shard_map/all_to_all | solution.py:79
  23.4 18.2 %all-gather.2.cloned.1.call-done = bf16[1024,1536]{1,0:T(8,128)(2,1)} async-done(((bf16[128,1536]{1,0:T(8,128)(2,1)}), bf16[1024,1536]{1,0:T(8,128)(2,1)}) %all-gather.2.cloned.1.call-update) | async-done | bytes 3145744 | tf_op jit(solution)/shard_map/all_gather | solution.py:18
  41.6 3.8 %fusion.36 = (bf16[1024,768]{1,0:T(8,128)(2,1)}, bf16[1024,768]{1,0:T(8,128)(2,1)}) fusion(bf16[1024,1536]{1,0:T(8,128)(2,1)} %all-gather.2.cloned.1.call-done), kind=kLoop, calls=%fused_computation.73 | loop fusion | bytes 6291456 | tf_op jit(solution)/shard_map/slice | solution.py:20
  45.4 25.6 %all-to-all-done = bf16[16,128,768]{2,1,0:T(8,128)(2,1)S(1)} async-done(((bf16[16,128,768]{2,1,0:T(8,128)(2,1)}), bf16[16,128,768]{2,1,0:T(8,128)(2,1)S(1)}, u32[]{:S(2)}, u32[]{:S(2)}) %all-to-all-start) | async-done | bytes 3145760 | tf_op jit(solution)/shard_map/all_to_all | solution.py:79
  71.0 14.5 %bitcast_reduce_fusion.1 = (f32[2048,2]{0,1:T(2,128)S(1)}, f32[2048,2]{0,1:T(2,128)S(1)}, f32[2048,2048]{0,1:T(8,128)}) fusion(bf16[2048,768]{1,0:T(8,128)(2,1)S(1)} %bitcast.65, bf16[1024,768]{1,0:T(8,128)(2,1)} %get-tuple-element.12, bf16[1024,768]{1,0:T(8,128)(2,1)} %get-tuple-element.11), kind=kOutput, calls=%fused_computation.15 | convolution fusion | flops 6465511424 | bytes 23101440 | tf_op jit(solution)/shard_map/dot_general | solution.py:87
  85.6 0.4 copy.16
  85.9 0.5 reshape.141
  86.4 0.4 copy.17
  86.8 0.5 reshape.143
  87.3 0.4 broadcast_in_dim.18
  87.7 14.6 %all_to_all.47 = f32[16,1,8192]{2,1,0:T(1,128)S(1)} all-to-all(f32[16,1,8192]{2,1,0:T(1,128)S(1)} %broadcast_in_dim.18), channel_id=1, replica_groups=mesh['row'=8,'col_0'=4,'col_1'=4] {'col_0','col_1'}, dimensions={0} | all-to-all | bytes 1048576 | tf_op jit(solution)/shard_map/all_to_all | solution.py:27
  102.3 0.3 reduce_sum.212
  102.7 1.0 div.96
  103.7 0.3 copy.20
  104.0 8.5 %fusion.5 = (f32[2048]{0:T(1024)S(1)}, f32[2048]{0:T(1024)S(1)}) fusion(f32[2048,2]{0,1:T(2,128)S(1)} %copy.20, f32[2048,2048]{0,1:T(8,128)} %get-tuple-element.19), kind=kLoop, calls=%fused_computation.9 | loop fusion | flops 20967424 | bytes 16809984 | tf_op jit(solution)/shard_map/reduce_sum | solution.py:101
  112.6 0.1 broadcast_in_dim.19
  112.6 10.4 %all_to_all.48 = f32[8,1,4096]{2,1,0:T(1,128)S(1)} all-to-all(f32[8,1,4096]{2,1,0:T(1,128)S(1)} %broadcast_in_dim.19), channel_id=1, replica_groups=mesh['row'=8,'col_0'=4,'col_1'=4] {'row'}, dimensions={0} | all-to-all | bytes 262144 | tf_op jit(solution)/shard_map/all_to_all | solution.py:27
  123.0 0.1 reduce_sum.215
  123.1 7.4 %fusion.6 = f32[2048,2]{0,1:T(2,128)S(1)} fusion(f32[2,1024]{1,0:T(2,128)S(1)} %div.98, f32[2048,2048]{0,1:T(8,128)} %get-tuple-element.19), kind=kLoop, calls=%fused_computation.16 | loop fusion | flops 12578816 | bytes 16801792 | tf_op jit(solution)/shard_map/reduce_sum | solution.py:107
  130.5 0.1 broadcast_in_dim.20
  130.6 11.6 %all_to_all.49 = f32[16,2048,2]{1,2,0:T(2,128)S(1)} all-to-all(f32[16,2048,2]{1,2,0:T(2,128)S(1)} %broadcast_in_dim.20), channel_id=1, replica_groups=mesh['row'=8,'col_0'=4,'col_1'=4] {'col_0','col_1'}, dimensions={0} | all-to-all | bytes 524288 | tf_op jit(solution)/shard_map/all_to_all | solution.py:27
  142.2 0.1 reduce_sum.217
  142.3 8.6 %fusion.4 = f32[2048]{0:T(1024)S(1)} fusion(f32[2048,2]{0,1:T(2,128)S(1)} %broadcast_divide_fusion.1, f32[2048,2048]{0,1:T(8,128)} %get-tuple-element.19), kind=kLoop, calls=%fused_computation.7 | loop fusion | flops 12580864 | bytes 16801792 | tf_op jit(solution)/shard_map/reduce_sum | solution.py:109
  151.0 8.0 %all_to_all.50 = f32[8,2,1024]{2,1,0:T(2,128)S(1)} all-to-all(f32[8,2,1024]{2,1,0:T(2,128)S(1)} %broadcast_in_dim.22), channel_id=1, replica_groups=mesh['row'=8,'col_0'=4,'col_1'=4] {'row'}, dimensions={0} | all-to-all | bytes 131072 | tf_op jit(solution)/shard_map/all_to_all | solution.py:27
  159.0 7.4 %fusion.7 = f32[2048,2]{0,1:T(2,128)S(1)} fusion(f32[2,1024]{1,0:T(2,128)S(1)} %broadcast_divide_fusion.3, f32[2048,2048]{0,1:T(8,128)} %get-tuple-element.19), kind=kLoop, calls=%fused_computation.17 | loop fusion | flops 12578816 | bytes 16801792 | tf_op jit(solution)/shard_map/reduce_sum | solution.py:107
  166.4 0.1 broadcast_in_dim.23
  166.5 11.6 %all_to_all.51 = f32[16,2048,2]{1,2,0:T(2,128)S(1)} all-to-all(f32[16,2048,2]{1,2,0:T(2,128)S(1)} %broadcast_in_dim.23), channel_id=1, replica_groups=mesh['row'=8,'col_0'=4,'col_1'=4] {'col_0','col_1'}, dimensions={0} | all-to-all | bytes 524288 | tf_op jit(solution)/shard_map/all_to_all | solution.py:27
  178.1 0.1 reduce_sum.221
  178.2 8.6 %fusion.10 = f32[2048]{0:T(1024)S(1)} fusion(f32[2048,2]{0,1:T(2,128)S(1)} %broadcast_divide_fusion, f32[2048,2048]{0,1:T(8,128)} %get-tuple-element.19), kind=kLoop, calls=%fused_computation.22 | loop fusion | flops 12580864 | bytes 16801792 | tf_op jit(solution)/shard_map/reduce_sum | solution.py:109
  186.8 8.0 %all_to_all.52 = f32[8,2,1024]{2,1,0:T(2,128)S(1)} all-to-all(f32[8,2,1024]{2,1,0:T(2,128)S(1)} %broadcast_in_dim.25), channel_id=1, replica_groups=mesh['row'=8,'col_0'=4,'col_1'=4] {'row'}, dimensions={0} | all-to-all | bytes 131072 | tf_op jit(solution)/shard_map/all_to_all | solution.py:27
  194.8 7.6 %fusion.9 = f32[2048,2]{0,1:T(2,128)S(1)} fusion(f32[2,1024]{1,0:T(2,128)S(1)} %broadcast_divide_fusion.2, f32[2048,2]{0,1:T(2,128)S(1)} %broadcast_divide_fusion, f32[2048,2048]{0,1:T(8,128)} %get-tuple-element.19), kind=kLoop, calls=%fused_computation.19 | loop fusion | flops 16773120 | bytes 16818176 | tf_op jit(solution)/shard_map/reduce_sum | solution.py:112
  202.4 0.8 broadcast_in_dim.26
  203.2 3.5 %all-to-all-start.7 = ((f32[16,2048,2]{1,2,0:T(2,128)}), f32[16,2048,2]{1,2,0:T(2,128)S(1)}, u32[]{:S(2)}, u32[]{:S(2)}) async-start(f32[16,2048,2]{1,2,0:T(2,128)} %broadcast_in_dim.26), calls=%async_computation.7 | async-start | bytes 524288 | tf_op jit(solution)/shard_map/all_to_all | solution.py:27
  206.8 0.3 reduce-scatter.3.cloned.1.call-start
  207.0 1.0 slice.58
  208.1 0.3 copy.19
  208.4 7.2 %all-to-all-done.7 = f32[16,2048,2]{1,2,0:T(2,128)S(1)} async-done(((f32[16,2048,2]{1,2,0:T(2,128)}), f32[16,2048,2]{1,2,0:T(2,128)S(1)}, u32[]{:S(2)}, u32[]{:S(2)}) %all-to-all-start.7) | async-done | bytes 262176 | tf_op jit(solution)/shard_map/all_to_all | solution.py:27
  215.6 0.1 reduce_sum.225
  215.7 12.1 %fusion.3 = bf16[2048,2048]{0,1:T(8,128)(2,1)S(1)} fusion(f32[2048,2048]{0,1:T(8,128)} %get-tuple-element.19, f32[2048]{0:T(1024)S(1)} %get-tuple-element.18, f32[2048]{0:T(1024)S(1)} %bitcast.68, f32[2048,2]{0,1:T(2,128)S(1)} %reduce_sum.225, f32[2048,2]{0,1:T(2,128)S(1)} %broadcast_divide_fusion, f32[2048,2]{0,1:T(2,128)S(1)} %copy.19), kind=kLoop, calls=%fused_computation.4 | loop fusion | flops 46137344 | bytes 25231360 | tf_op jit(solution)/shard_map/convert_element_type | solution.py:119
  227.9 3.2 %copy-done = bf16[2048,2048]{0,1:T(8,128)(2,1)} copy-done((bf16[2048,2048]{0,1:T(8,128)(2,1)}, bf16[2048,2048]{0,1:T(8,128)(2,1)S(1)}, u32[]{:S(2)}) %copy-start) | copy-done | bytes 8388632
  231.1 8.6 %multiply_convert_fusion = bf16[2048,768]{1,0:T(8,128)(2,1)} fusion(bf16[2048,2048]{0,1:T(8,128)(2,1)S(1)} %fusion.3, bf16[1024,768]{1,0:T(8,128)(2,1)S(1)} %copy-done.6, bf16[1024,768]{1,0:T(8,128)(2,1)S(1)} %copy-done.5), kind=kOutput, calls=%fused_computation.27 | convolution fusion | flops 6451888128 | bytes 14680064 | tf_op jit(solution)/shard_map/dot_general | solution.py:122
  239.7 4.4 %fusion.35 = (bf16[2048,1024]{0,1:T(8,128)(2,1)S(1)}, bf16[2048,1024]{0,1:T(8,128)(2,1)S(1)}) fusion(bf16[2048,2048]{0,1:T(8,128)(2,1)} %copy-done), kind=kLoop, calls=%fused_computation.72 | loop fusion | bytes 16777216 | tf_op jit(solution)/shard_map/slice | solution.py:124
  244.1 3.4 %fusion.38 = f32[8,128,768]{2,1,0:T(8,128)S(1)} fusion(bf16[8,128,2048]{2,1,0:T(8,128)(2,1)S(1)} %bitcast.64, bf16[2048,768,1]{1,0,2:T(8,128)(2,1)S(1)} %bitcast.66), kind=kOutput, calls=%fused_computation.75 | convolution fusion | flops 3221225472 | bytes 10485760 | tf_op jit(solution)/shard_map/dot_general | solution.py:129
  247.5 3.4 %fusion.39 = f32[8,128,768]{2,1,0:T(8,128)S(1)} fusion(bf16[8,128,2048]{2,1,0:T(8,128)(2,1)S(1)} %bitcast.63, bf16[2048,768,1]{1,0,2:T(8,128)(2,1)S(1)} %bitcast.67), kind=kOutput, calls=%fused_computation.76 | convolution fusion | flops 3221225472 | bytes 10485760 | tf_op jit(solution)/shard_map/dot_general | solution.py:132
  251.0 2.4 fusion.12
  253.3 3.7 %all-to-all-start.8 = ((bf16[8,128,1536]{2,1,0:T(8,128)(2,1)}), bf16[8,128,1536]{2,1,0:T(8,128)(2,1)S(1)}, u32[]{:S(2)}, u32[]{:S(2)}) async-start(bf16[8,128,1536]{2,1,0:T(8,128)(2,1)} %fusion.12), calls=%async_computation.10 | async-start | bytes 6291456 | tf_op jit(solution)/shard_map/all_to_all | solution.py:60
  257.0 0.0 reduce-scatter.5.cloned.1.call-start
  257.1 16.8 %reduce-scatter.3.cloned.1.call-done = bf16[512,768]{1,0:T(8,128)(2,1)} async-done(((bf16[2048,768]{1,0:T(8,128)(2,1)}), bf16[512,768]{1,0:T(8,128)(2,1)}) %reduce-scatter.3.cloned.1.call-update) | async-done | bytes 786448 | tf_op jit(solution)/shard_map/reduce_scatter | solution.py:48
  273.9 21.4 %all-to-all-done.8 = bf16[8,128,1536]{2,1,0:T(8,128)(2,1)S(1)} async-done(((bf16[8,128,1536]{2,1,0:T(8,128)(2,1)}), bf16[8,128,1536]{2,1,0:T(8,128)(2,1)S(1)}, u32[]{:S(2)}, u32[]{:S(2)}) %all-to-all-start.8) | async-done | bytes 3145760 | tf_op jit(solution)/shard_map/all_to_all | solution.py:60
  295.3 0.4 convert_reduce_fusion
  295.8 0.3 fusion.27
  296.0 1.1 fusion.29
  297.1 1.3 reduce-scatter.5.cloned.1.call-done
  298.5 1.2 fusion.31
  299.7 2.0 fusion.32
  (35 shorter events, 0.3 us)
Async XLA Ops:
  7.2 34.5 %all-gather.2.cloned.1.call-start = ((), (), s32[]{:S(2)}) async-start(), calls=%async_computation.11 | async-start | bytes 3538944 | tf_op jit(solution)/shard_map/all_gather | solution.py:18
  15.4 55.6 %all-to-all-start = ((bf16[16,128,768]{2,1,0:T(8,128)(2,1)}), bf16[16,128,768]{2,1,0:T(8,128)(2,1)S(1)}, u32[]{:S(2)}, u32[]{:S(2)}) async-start(bf16[16,128,768]{2,1,0:T(8,128)(2,1)} %stack.2), calls=%async_computation | async-start | bytes 6291456 | tf_op jit(solution)/shard_map/all_to_all | solution.py:79
  71.0 14.5 %copy-start.1 = (bf16[16,128,768]{2,1,0:T(8,128)(2,1)}, bf16[16,128,768]{2,1,0:T(8,128)(2,1)S(1)}, u32[]{:S(2)}) copy-start(bf16[16,128,768]{2,1,0:T(8,128)(2,1)S(1)} %all-to-all-done) | copy-start | bytes 9437188
  203.2 12.4 %all-to-all-start.7 = ((f32[16,2048,2]{1,2,0:T(2,128)}), f32[16,2048,2]{1,2,0:T(2,128)S(1)}, u32[]{:S(2)}, u32[]{:S(2)}) async-start(f32[16,2048,2]{1,2,0:T(2,128)} %broadcast_in_dim.26), calls=%async_computation.7 | async-start | bytes 524288 | tf_op jit(solution)/shard_map/all_to_all | solution.py:27
  206.8 67.1 %reduce-scatter.3.cloned.1.call-start = ((), (), s32[]{:S(2)}) async-start(), calls=%async_computation.12 | async-start | bytes 3932160 | tf_op jit(solution)/shard_map/reduce_scatter | solution.py:48
  215.7 15.4 %copy-start.5 = (bf16[1024,768]{1,0:T(8,128)(2,1)S(1)}, bf16[1024,768]{1,0:T(8,128)(2,1)}, u32[]{:S(2)}) copy-start(bf16[1024,768]{1,0:T(8,128)(2,1)} %get-tuple-element.11) | copy-start | bytes 4718596
  215.7 15.4 %copy-start.6 = (bf16[1024,768]{1,0:T(8,128)(2,1)S(1)}, bf16[1024,768]{1,0:T(8,128)(2,1)}, u32[]{:S(2)}) copy-start(bf16[1024,768]{1,0:T(8,128)(2,1)} %get-tuple-element.12) | copy-start | bytes 4718596
  227.8 3.2 %copy-start = (bf16[2048,2048]{0,1:T(8,128)(2,1)}, bf16[2048,2048]{0,1:T(8,128)(2,1)S(1)}, u32[]{:S(2)}) copy-start(bf16[2048,2048]{0,1:T(8,128)(2,1)S(1)} %fusion.3) | copy-start | bytes 25165828
  239.7 4.4 %copy-start.2 = (bf16[16,128,768]{2,1,0:T(8,128)(2,1)S(1)}, bf16[16,128,768]{2,1,0:T(8,128)(2,1)}, u32[]{:S(2)}) copy-start(bf16[16,128,768]{2,1,0:T(8,128)(2,1)} %copy-done.1) | copy-start | bytes 9437188
  250.9 44.8 %copy-start.3 = (bf16[128,768]{1,0:T(8,128)(2,1)S(1)}, bf16[128,768]{1,0:T(8,128)(2,1)}, u32[]{:S(2)}) copy-start(bf16[128,768]{1,0:T(8,128)(2,1)} %param.5) | copy-start | bytes 589828
  251.0 44.8 %copy-start.4 = (bf16[128,768]{1,0:T(8,128)(2,1)S(1)}, bf16[128,768]{1,0:T(8,128)(2,1)}, u32[]{:S(2)}) copy-start(bf16[128,768]{1,0:T(8,128)(2,1)} %param.4) | copy-start | bytes 589828
  253.3 42.0 %all-to-all-start.8 = ((bf16[8,128,1536]{2,1,0:T(8,128)(2,1)}), bf16[8,128,1536]{2,1,0:T(8,128)(2,1)S(1)}, u32[]{:S(2)}, u32[]{:S(2)}) async-start(bf16[8,128,1536]{2,1,0:T(8,128)(2,1)} %fusion.12), calls=%async_computation.10 | async-start | bytes 6291456 | tf_op jit(solution)/shard_map/all_to_all | solution.py:60
  257.0 41.5 %reduce-scatter.5.cloned.1.call-start = ((), (), s32[]{:S(2)}) async-start(), calls=%async_computation.13 | async-start | bytes 983040 | tf_op jit(solution)/shard_map/reduce_scatter | solution.py:48
Sparse Core Ops, SparseCore 0:
  11.4 30.1 all-gather.1
  239.8 34.0 reduce-scatter.2
  276.3 22.1 reduce-scatter.4
